TPU v7x, 256 devices: a whole 4x4x8 slice. The times are simulated.
256 devices in a mesh: dom: 16 (over z, y_lo), edge: 16 (over x, y_hi, core).
Axes of the slice: x: 4, y: 4 (y_hi: 2, y_lo: 2; y = y_hi * 2 + y_lo), z: 8, core: 2. Of those that a mesh axis runs over, the one named last changes fastest.
Arguments:
- src_table: float32 [4096, 400], P(('dom', 'edge')), may hold values from -6 to 6
- src_state: float32 [4096], P(('dom', 'edge')), may hold values from 0.1 to 30
- dst_table: float32 [4096, 400], P(('dom', 'edge')), may hold values from -6 to 6
- dst_state: float32 [4096], P(('dom', 'edge')), may hold values from 0.1 to 30
- relations: float32 [4131, 400], replicated, may hold values from -1.5 to 1.5
- edge_src: int32 [2, 128000], P(None, ('dom', 'edge')), may hold values from 0 to 255
- edge_rel: int32 [2, 128000], P(None, ('dom', 'edge')), may hold values from 0 to 4130
- edge_dst: int32 [2, 128000], P(None, ('dom', 'edge')), may hold values from 0 to 255
- negatives: int32 [2, 256, 500], P(None, ('dom', 'edge')), may hold values from 0 to 255
Outputs:
- src_out: float32 [4096, 400], P(('dom', 'edge'))
- src_state_out: float32 [4096], P(('dom', 'edge'))
- dst_out: float32 [4096, 400], P(('dom', 'edge'))
- dst_state_out: float32 [4096], P(('dom', 'edge'))
All inputs are finite; a program needn't handle non-finite values.
Results may differ from a plain program's by a relative error of at most 0.00013.
Values sent between devices are 32-bit elements; how exact they have to be, the bound alone decides.
A program may use at most 64 MiB of HBM per device.

v0:
```python
import functools

import jax
import jax.numpy as jnp
from jax import lax
from jax.experimental import pallas as pl
from jax.experimental.pallas import tpu as pltpu
from jax.sharding import PartitionSpec as P

MESH = pl.DeviceIdType.MESH
LEARN_RATE = 0.1
EPSILON = 1e-06
BF = jnp.bfloat16
F32 = jnp.float32


def up(n, m):
    return (n + m - 1) // m * m


def halves(x):
    hi = x.astype(BF)
    return hi, (x - hi.astype(F32)).astype(BF)


def nn(a, b):
    return jnp.dot(a, b, preferred_element_type=F32)


def nt(a, b):
    return lax.dot_general(a, b, (((1,), (1,)), ((), ())), preferred_element_type=F32)


def kernel(
    doms, chips, half,
    src_ref, sst_ref, dst_ref, dstt_ref, rel_hbm, es_ref, er_ref, ed_ref, ng_ref,
    src_out, sst_out, dst_out, dstt_out,
    rel_v, raw, rsp, hot, hot_t, wgt, pos, ids,
    own_s, own_d, full_s, full_d, part_s, part_d, sib_s, sib_d, sum_s, sum_d, red_s, red_d,
    qh, ql, dh, dl, th, tl, wth, wtl, wh, wl,
    rel_sem, ags_send, ags_recv, agd_send, agd_recv, fws_send, fws_recv, fwd_send, fwd_recv,
    dd_send, dd_recv, rss_send, rss_recv, rsd_send, rsd_recv,
):
    rows = src_ref.shape[0]
    width = src_ref.shape[1]
    hp = up(half, 128)
    wide = 2 * hp
    ents = full_s.shape[1]
    hent = ents // 2
    edges = es_ref.shape[1]
    ep = rsp.shape[1]
    nrel = rel_v.shape[0]
    shift = hp - half

    dom = lax.axis_index("dom")
    k = lax.axis_index("edge")
    core = lax.rem(k, 2)
    chip = lax.div(k, 2)
    mate = chip * 2 + (1 - core)

    def at_dom(step):
        return lax.rem(dom + step + doms, doms)

    def peer(j):
        return lax.rem(chip + j, chips)

    piece = up(-(-nrel // rel_sem.shape[0]), 8)
    rel_copies = []
    for n in range(rel_sem.shape[0]):
        lo = n * piece
        size = min(piece, nrel - lo)
        c = pltpu.make_async_copy(rel_hbm.at[pl.ds(lo, size)], rel_v.at[pl.ds(lo, size)], rel_sem.at[n])
        c.start()
        rel_copies.append(c)

    bar = pltpu.get_barrier_semaphore()
    count = 1
    pl.semaphore_signal(bar, inc=1, device_id=(dom, mate), device_id_type=MESH)
    for j in range(1, chips):
        pl.semaphore_signal(bar, inc=1, device_id=(dom, peer(j) * 2 + core), device_id_type=MESH)
        count += 1
    for other in (at_dom(1), at_dom(-1)):
        for j in range(chips):
            pl.semaphore_signal(bar, inc=1, device_id=(other, peer(j) * 2 + core), device_id_type=MESH)
            count += 1

    lane = lax.broadcasted_iota(jnp.int32, (rows, wide), 1)

    def spread(x_ref, to):
        to[0] = jnp.zeros((rows, wide), F32)
        to[0, :, 0:width] = x_ref[...]
        x = to[0]
        im = pltpu.roll(x, shift, axis=1)
        to[0] = jnp.where(lane < half, x, jnp.where(lane >= hp, im, 0.0))

    def joined(x):
        im = pltpu.roll(x, wide - shift, axis=1)
        return jnp.where(lane < half, x, im)[:, :width]

    spread(src_ref, own_s)
    spread(dst_ref, own_d)

    eye = lax.broadcasted_iota(jnp.int32, (rows, rows), 0) == lax.broadcasted_iota(jnp.int32, (rows, rows), 1)

    def column(x_ref):
        return jnp.sum(jnp.where(eye, jnp.broadcast_to(x_ref[...], (rows, rows)), 0.0), axis=1, keepdims=True)

    def as_row(x):
        return jnp.sum(jnp.where(eye, jnp.broadcast_to(x, (rows, rows)), 0.0), axis=0, keepdims=True)

    src_state = column(sst_ref)
    dst_state = column(dstt_ref)

    my_rows = pl.ds(pl.multiple_of(core * hent + chip * rows, rows), rows)

    def block_of(c):
        return pl.ds(pl.multiple_of(core * hent + c * rows, rows), rows)

    def mate_block_of(c):
        return pl.ds(pl.multiple_of((1 - core) * hent + c * rows, rows), rows)

    def gather_src(step):
        out = []
        for j in list(range(1, chips)):
            c = pltpu.make_async_remote_copy(
                own_s.at[step], full_s.at[step, my_rows], ags_send.at[step, j], ags_recv.at[step, chip],
                device_id=(dom, peer(j) * 2 + core), device_id_type=MESH)
            c.start()
            out.append(c)
        c = pltpu.make_async_remote_copy(
            own_s.at[step], full_s.at[step, my_rows], fws_send.at[step, chip], fws_recv.at[step, chip],
            device_id=(dom, mate), device_id_type=MESH)
        c.start()
        out.append(c)
        full_s[step, my_rows] = own_s[step]
        return out

    def gather_dst(step):
        out = []
        for j in range(chips):
            c = pltpu.make_async_remote_copy(
                own_d.at[step], full_d.at[step, my_rows], agd_send.at[step, j], agd_recv.at[step, chip],
                device_id=(at_dom(step + 1), peer(j) * 2 + core), device_id_type=MESH)
            c.start()
            out.append(c)
        return out

    def forward(step, full, recv, fsend, frecv, first):
        out = []
        for j in range(first, chips):
            c = peer(j)
            blk = full.at[step, block_of(c)]
            pltpu.make_async_copy(blk, blk, recv.at[step, c]).wait()
            f = pltpu.make_async_remote_copy(
                blk, blk, fsend.at[step, c], frecv.at[step, c], device_id=(dom, mate), device_id_type=MESH)
            f.start()
            out.append(f)
        return out

    def from_mate(step, full, frecv):
        for c in range(chips):
            blk = full.at[step, mate_block_of(c)]
            pltpu.make_async_copy(blk, blk, frecv.at[step, c]).wait()

    def place(x):
        per = rows * 2
        return lax.rem(lax.div(x, rows), 2) * hent + lax.div(x, per) * rows + lax.rem(x, rows)

    def prepare(step):
        raw[pl.ds(edges // 8 * 8, ep - edges // 8 * 8)] = jnp.zeros((ep - edges // 8 * 8, wide), F32)
        unroll = 20

        def body(b, carry):
            for u in range(unroll):
                e = b * unroll + u
                i = er_ref[step, e]
                raw[pl.ds(e, 1), 0:width] = rel_v[pl.ds(i, 1), :]
            return carry

        lax.fori_loop(0, edges // unroll, body, 0)
        for m in range(0, ep, 128):
            x = raw[m:m + 128]
            ln = lax.broadcasted_iota(jnp.int32, (128, wide), 1)
            im = pltpu.roll(x, shift, axis=1)
            rsp[step, m:m + 128] = jnp.where(ln < half, x, jnp.where((ln >= hp) & (ln < hp + half), im, 0.0))

        def hots(ref, slot):
            ids[slot] = jnp.full((1, ep), -1, jnp.int32)
            ids[slot, :, 0:edges] = ref[step:step + 1, :]
            x = ids[slot]
            x = jnp.where(x < 0, -1, place(jnp.maximum(x, 0)))
            return x

        xs, xd, xn = hots(es_ref, 0), hots(ed_ref, 1), hots(ng_ref, 2)
        for m in range(0, ents, 128):
            line = lax.broadcasted_iota(jnp.int32, (128, ep), 0) + m
            s = jnp.where(line == xs, 1.0, 0.0)
            hot_t[step, m:m + 128] = s.astype(BF)
            hot[step, :, m:m + 128] = s.T.astype(BF)
            d = jnp.where(line == xd, 1.0, 0.0)
            c = jnp.sum(jnp.where(line == xn, 1.0, 0.0), axis=1, keepdims=True)
            pos[step, m:m + 128] = d
            wgt[step, m:m + 128] = d + c

    def split_to(ref, step, a, b):
        for m in range(0, ents, 128):
            a[m:m + 128], b[m:m + 128] = halves(ref[step, m:m + 128])

    def rotated(step):
        split_to(full_s, step, th, tl)
        for m in range(0, ep, 128):
            o = hot[step, m:m + 128]
            s = nn(o, th[...]) + nn(o, tl[...])
            sr, si = s[:, :hp], s[:, hp:]
            rr, ri = rsp[step, m:m + 128, :hp], rsp[step, m:m + 128, hp:]
            qh[m:m + 128, :hp], ql[m:m + 128, :hp] = halves(sr * rr - si * ri)
            qh[m:m + 128, hp:], ql[m:m + 128, hp:] = halves(sr * ri + si * rr)

    def weights(step):
        split_to(full_d, step, dh, dl)
        for m in range(0, ents, 128):
            a, b = dh[m:m + 128], dl[m:m + 128]
            s = nt(a, qh[...]) + (nt(a, ql[...]) + nt(b, qh[...]))
            w = jax.nn.sigmoid(s) * wgt[step, m:m + 128] - pos[step, m:m + 128]
            wth[m:m + 128], wtl[m:m + 128] = halves(w)
            wh[:, m:m + 128], wl[:, m:m + 128] = halves(w.T)

    lower = pl.ds(pl.multiple_of(core * hent, hent), hent)
    upper = pl.ds(pl.multiple_of((1 - core) * hent, hent), hent)

    def dst_part(which):
        a, b = wth[which], wtl[which]
        return nn(a, qh[...]) + (nn(a, ql[...]) + nn(b, qh[...]))

    def edge_grads(step):
        for m in range(0, ep, 128):
            a, b = wh[m:m + 128], wl[m:m + 128]
            g = nn(a, dh[...]) + (nn(a, dl[...]) + nn(b, dh[...]))
            gr, gi = g[:, :hp], g[:, hp:]
            rr, ri = rsp[step, m:m + 128, :hp], rsp[step, m:m + 128, hp:]
            qh[m:m + 128, :hp], ql[m:m + 128, :hp] = halves(gr * rr + gi * ri)
            qh[m:m + 128, hp:], ql[m:m + 128, hp:] = halves(gi * rr - gr * ri)

    def src_part(step, which):
        o = hot_t[step, which]
        return nn(o, qh[...]) + nn(o, ql[...])

    def to_mate(step, t, part, sib):
        c = pltpu.make_async_remote_copy(
            part.at[step], sib.at[step], dd_send.at[step, t], dd_recv.at[step, t],
            device_id=(dom, mate), device_id_type=MESH)
        c.start()
        return c

    def to_owners(step, t, copy, mine, sib, total, red, send, recv, target, first):
        copy.wait_recv()
        total[step] = mine + sib[step]
        out = []
        for j in range(first, chips):
            c = peer(j)
            r = pltpu.make_async_remote_copy(
                total.at[step, pl.ds(pl.multiple_of(c * rows, rows), rows)], red.at[step, chip],
                send.at[step, j], recv.at[step, chip],
                device_id=(target, c * 2 + core), device_id_type=MESH)
            r.start()
            out.append(r)
        if first == 1:
            red[step, chip] = total[step, pl.ds(pl.multiple_of(chip * rows, rows), rows)]
        return out

    def arrived(step, red, recv, first):
        for j in range(first, chips):
            blk = red.at[step, peer(j)]
            pltpu.make_async_copy(blk, blk, recv.at[step, peer(j)]).wait()
        g = red[step, 0]
        for c in range(1, chips):
            g = g + red[step, c]
        return g

    def adagrad(table, state, g):
        state = state + jnp.sum(g * g, axis=1, keepdims=True) / width
        return table - LEARN_RATE * g / (jnp.sqrt(state) + EPSILON), state

    pl.semaphore_wait(bar, count)

    sent = []
    sent += gather_src(0)
    sent += gather_dst(0)
    for c in rel_copies:
        c.wait()
    raw[...] = jnp.zeros((ep, wide), F32)
    prepare(0)

    for step in range(2):
        sent += forward(step, full_s, ags_recv, fws_send, fws_recv, 1)
        sent += forward(step, full_d, agd_recv, fwd_send, fwd_recv, 0)
        from_mate(step, full_s, fws_recv)
        rotated(step)
        from_mate(step, full_d, fwd_recv)
        weights(step)
        part_d[step] = dst_part(upper)
        cd = to_mate(step, 0, part_d, sib_d)
        mine_d = dst_part(lower)
        sent += to_owners(step, 0, cd, mine_d, sib_d, sum_d, red_d, rsd_send, rsd_recv, at_dom(-step - 1), 0)
        edge_grads(step)
        part_s[step] = src_part(step, upper)
        cs = to_mate(step, 1, part_s, sib_s)
        mine_s = src_part(step, lower)
        sent += to_owners(step, 1, cs, mine_s, sib_s, sum_s, red_s, rss_send, rss_recv, dom, 1)
        if step == 0:
            prepare(1)
        g = arrived(step, red_d, rsd_recv, 0)
        table, dst_state = adagrad(own_d[step], dst_state, g)
        if step == 0:
            own_d[1] = table
            sent += gather_dst(1)
        else:
            dst_out[...] = joined(table)
            dstt_out[...] = as_row(dst_state)
        g = arrived(step, red_s, rss_recv, 1)
        table, src_state = adagrad(own_s[step], src_state, g)
        if step == 0:
            own_s[1] = table
            sent += gather_src(1)
        else:
            src_out[...] = joined(table)
            sst_out[...] = as_row(src_state)
        sent += [cd, cs]
    for c in sent:
        c.wait_send()


def solution(mesh):
    doms, edge_axis = mesh.shape["dom"], mesh.shape["edge"]
    chips = edge_axis // 2

    def on_device(
        src_table, src_state, dst_table, dst_state, relations, edge_src, edge_rel, edge_dst, negatives
    ):
        rows, width = src_table.shape
        half = width // 2
        wide = 2 * up(half, 128)
        ents = rows * edge_axis
        edges = edge_src.shape[1]
        ep = up(edges, 128)
        nrel = relations.shape[0]
        vm, dma = pltpu.VMEM, pltpu.SemaphoreType.DMA
        in_vmem = pl.BlockSpec(memory_space=pltpu.VMEM)
        shard = jax.ShapeDtypeStruct((rows, width), F32)
        line = jax.ShapeDtypeStruct((1, rows), F32)
        out = pl.pallas_call(
            functools.partial(kernel, doms, chips, half),
            out_shape=(shard, line, shard, line),
            in_specs=[in_vmem] * 4
            + [pl.BlockSpec(memory_space=pl.ANY), in_vmem, pl.BlockSpec(memory_space=pltpu.SMEM)]
            + [in_vmem] * 2,
            out_specs=(in_vmem,) * 4,
            scratch_shapes=[
                vm((nrel, width), F32),
                vm((ep, wide), F32),
                vm((2, ep, wide), F32),
                vm((2, ep, ents), BF),
                vm((2, ents, ep), BF),
                vm((2, ents, ep), F32),
                vm((2, ents, ep), F32),
                vm((3, 1, ep), jnp.int32),
            ]
            + [vm((2, rows, wide), F32)] * 2
            + [vm((2, ents, wide), F32)] * 2
            + [vm((2, ents // 2, wide), F32)] * 6
            + [vm((2, chips, rows, wide), F32)] * 2
            + [vm((ep, wide), BF)] * 2
            + [vm((ents, wide), BF)] * 4
            + [vm((ents, ep), BF)] * 2
            + [vm((ep, ents), BF)] * 2
            + [dma((8,))]
            + [dma((2, chips))] * 8
            + [dma((2, 2))] * 2
            + [dma((2, chips))] * 4,
            compiler_params=pltpu.CompilerParams(
                collective_id=0, has_side_effects=True, vmem_limit_bytes=60 * 1024 * 1024
            ),
        )(
            src_table,
            src_state.reshape(1, rows),
            dst_table,
            dst_state.reshape(1, rows),
            relations,
            edge_src,
            edge_rel,
            edge_dst,
            negatives.reshape(2, edges),
        )
        return out[0], out[1].reshape(rows), out[2], out[3].reshape(rows)

    return jax.shard_map(
        on_device,
        mesh=mesh,
        in_specs=(
            P(("dom", "edge"), None),
            P(("dom", "edge")),
            P(("dom", "edge"), None),
            P(("dom", "edge")),
            P(),
            P(None, ("dom", "edge")),
            P(None, ("dom", "edge")),
            P(None, ("dom", "edge")),
            P(None, ("dom", "edge"), None),
        ),
        out_specs=(
            P(("dom", "edge"), None),
            P(("dom", "edge")),
            P(("dom", "edge"), None),
            P(("dom", "edge")),
        ),
        check_vma=False,
    )
```

profile of v0, /device:TPU:1, one launch (start us, length us, event | category | flops | bytes accessed | tf_op | source)
XLA Modules:
  0.0 73.8 jit_solution(16472201972933070892)
XLA Ops:
  0.6 1.3 %copy.16 = s32[2,1,500]{2,0,1:T(2,128)} copy(s32[2,1,500]{2,1,0:T(1,128)} %param.17) | data formatting | bytes 8000
  1.9 8.6 %copy.13.rel_hbm = f32[4131,400]{1,0:T(8,128)} copy(f32[4131,400]{0,1:T(8,128)} %param.13) | data formatting | bytes 13219200 | tf_op args[4]
  10.5 58.2 %shard_map.120 = (f32[16,400]{1,0:T(8,128)}, f32[1,16]{1,0:T(1,128)}, f32[16,400]{1,0:T(8,128)}, f32[1,16]{1,0:T(1,128)}) custom-call(f32[16,400]{1,0:T(8,128)} %src_ref.1, f32[1,16]{1,0:T(1,128)} %bitcast.8, f32[16,400]{1,0:T(8,128)} %dst_ref.1, f32[1,16]{1,0:T(1,128)} %bitcast.9, f32[4131,400]{1,0:T(8,128)} %copy.13.rel_hbm, s32[2,500]{1,0:T(2,128)} %es_ref.1, ...), custom_call_target="tpu_custom_call" | custom-call | tf_op jit(solution)/shard_map/pallas_call | solution.py:351
  68.7 1.4 %copy.21 = f32[16,400]{1,0:T(8,128)} copy(f32[16,400]{1,0:T(8,128)} %get-tuple-element.16) | data formatting | bytes 51200
  70.1 1.2 %copy.22 = f32[16]{0:T(128)} copy(f32[16]{0:T(128)} %bitcast.11) | data formatting | bytes 128
  71.2 1.4 %copy.23 = f32[16,400]{1,0:T(8,128)} copy(f32[16,400]{1,0:T(8,128)} %get-tuple-element.18) | data formatting | bytes 51200
  72.6 1.2 %copy.24 = f32[16]{0:T(128)} copy(f32[16]{0:T(128)} %bitcast.10) | data formatting | bytes 128
where the time goes:
time: 74.3 us; the launch traced here: 73.8 us
  Pallas kernels  58.2 us (78%)
  local copies, waits for them, and re-layouts  14.9 us (20%)
    pallas_call x1, Pallas kernels, on_device(): pl.pallas_call(functools.partial(kernel, doms, chips, half), out_shape=(s...  58.2 us
    unnamed x6, local copies, waits for them, and re-layouts  14.9 us

commit v1 on v0

--- a/solution.py
+++ b/solution.py
@@ -34,8 +34,8 @@
 def kernel(
     doms, chips, half,
     src_ref, sst_ref, dst_ref, dstt_ref, rel_hbm, es_ref, er_ref, ed_ref, ng_ref,
-    src_out, sst_out, dst_out, dstt_out,
-    rel_v, raw, rsp, hot, hot_t, wgt, pos, ids,
+    out_ref,
+    rel_t, rel_e, rel_v, rsp, hot, hot_t, wgt, pos, ids,
     own_s, own_d, full_s, full_d, part_s, part_d, sib_s, sib_d, sum_s, sum_d, red_s, red_d,
     qh, ql, dh, dl, th, tl, wth, wtl, wh, wl,
     rel_sem, ags_send, ags_recv, agd_send, agd_recv, fws_send, fws_recv, fwd_send, fwd_recv,
@@ -49,7 +49,7 @@
     hent = ents // 2
     edges = es_ref.shape[1]
     ep = rsp.shape[1]
-    nrel = rel_v.shape[0]
+    nrel = rel_hbm.shape[1]
     shift = hp - half
 
     dom = lax.axis_index("dom")
@@ -64,14 +64,16 @@
     def peer(j):
         return lax.rem(chip + j, chips)
 
-    piece = up(-(-nrel // rel_sem.shape[0]), 8)
+    piece = up(-(-width // rel_sem.shape[0]), 8)
     rel_copies = []
     for n in range(rel_sem.shape[0]):
         lo = n * piece
-        size = min(piece, nrel - lo)
-        c = pltpu.make_async_copy(rel_hbm.at[pl.ds(lo, size)], rel_v.at[pl.ds(lo, size)], rel_sem.at[n])
-        c.start()
-        rel_copies.append(c)
+        size = min(piece, width - lo)
+        if size > 0:
+            c = pltpu.make_async_copy(
+                rel_hbm.at[pl.ds(lo, size)], rel_t.at[pl.ds(lo, size)], rel_sem.at[n])
+            c.start()
+            rel_copies.append(c)
 
     bar = pltpu.get_barrier_semaphore()
     count = 1
@@ -92,10 +94,6 @@
         x = to[0]
         im = pltpu.roll(x, shift, axis=1)
         to[0] = jnp.where(lane < half, x, jnp.where(lane >= hp, im, 0.0))
-
-    def joined(x):
-        im = pltpu.roll(x, wide - shift, axis=1)
-        return jnp.where(lane < half, x, im)[:, :width]
 
     spread(src_ref, own_s)
     spread(dst_ref, own_d)
@@ -166,27 +164,42 @@
         per = rows * 2
         return lax.rem(lax.div(x, rows), 2) * hent + lax.div(x, per) * rows + lax.rem(x, rows)
 
+    def turn_relations():
+        fill = jnp.zeros((hp - half, 128), F32)
+        full = nrel // 128
+
+        def turned(ref, cols, to):
+            rel_v[to, 0:hp] = jnp.concatenate([ref[0:half, cols], fill], axis=0).T
+            rel_v[to, hp:wide] = jnp.concatenate([ref[half:width, cols], fill], axis=0).T
+
+        def body(b, carry):
+            cols = pl.ds(pl.multiple_of(b * 128, 128), 128)
+            turned(rel_t, cols, cols)
+            return carry
+
+        lax.fori_loop(0, full, body, 0)
+        if nrel % 128:
+            rel_e[...] = jnp.zeros((width, 128), F32)
+            rel_e[:, 0:nrel % 128] = rel_t[:, full * 128:nrel]
+            turned(rel_e, slice(0, 128), slice(full * 128, full * 128 + 128))
+
     def prepare(step):
-        raw[pl.ds(edges // 8 * 8, ep - edges // 8 * 8)] = jnp.zeros((ep - edges // 8 * 8, wide), F32)
+        tail = edges // 8 * 8
+        rsp[step, tail:ep] = jnp.zeros((ep - tail, wide), F32)
         unroll = 20
 
         def body(b, carry):
             for u in range(unroll):
                 e = b * unroll + u
                 i = er_ref[step, e]
-                raw[pl.ds(e, 1), 0:width] = rel_v[pl.ds(i, 1), :]
+                rsp[step, pl.ds(e, 1), :] = rel_v[pl.ds(i, 1), :]
             return carry
 
         lax.fori_loop(0, edges // unroll, body, 0)
-        for m in range(0, ep, 128):
-            x = raw[m:m + 128]
-            ln = lax.broadcasted_iota(jnp.int32, (128, wide), 1)
-            im = pltpu.roll(x, shift, axis=1)
-            rsp[step, m:m + 128] = jnp.where(ln < half, x, jnp.where((ln >= hp) & (ln < hp + half), im, 0.0))
 
         def hots(ref, slot):
             ids[slot] = jnp.full((1, ep), -1, jnp.int32)
-            ids[slot, :, 0:edges] = ref[step:step + 1, :]
+            ids[slot, :, 0:edges] = ref[step] if len(ref.shape) == 3 else ref[step:step + 1, :]
             x = ids[slot]
             x = jnp.where(x < 0, -1, place(jnp.maximum(x, 0)))
             return x
@@ -288,7 +301,7 @@
     sent += gather_dst(0)
     for c in rel_copies:
         c.wait()
-    raw[...] = jnp.zeros((ep, wide), F32)
+    turn_relations()
     prepare(0)
 
     for step in range(2):
@@ -315,19 +328,31 @@
             own_d[1] = table
             sent += gather_dst(1)
         else:
-            dst_out[...] = joined(table)
-            dstt_out[...] = as_row(dst_state)
+            out_ref[rows:2 * rows] = table
+            out_ref[2 * rows + 1:2 * rows + 2, 0:rows] = as_row(dst_state)
         g = arrived(step, red_s, rss_recv, 1)
         table, src_state = adagrad(own_s[step], src_state, g)
         if step == 0:
             own_s[1] = table
             sent += gather_src(1)
         else:
-            src_out[...] = joined(table)
-            sst_out[...] = as_row(src_state)
+            out_ref[0:rows] = table
+            out_ref[2 * rows:2 * rows + 1, 0:rows] = as_row(src_state)
         sent += [cd, cs]
     for c in sent:
         c.wait_send()
+
+
+def finish(half, res_ref, src_out, sst_out, dst_out, dstt_out):
+    rows, width = src_out.shape
+    wide = res_ref.shape[1]
+    lane = lax.broadcasted_iota(jnp.int32, (rows, wide), 1)
+    for first, out in ((0, src_out), (rows, dst_out)):
+        x = res_ref[first:first + rows]
+        im = pltpu.roll(x, wide // 2 + half, axis=1)
+        out[...] = jnp.where(lane < half, x, im)[:, :width]
+    sst_out[...] = res_ref[2 * rows:2 * rows + 1, 0:rows]
+    dstt_out[...] = res_ref[2 * rows + 1:2 * rows + 2, 0:rows]
 
 
 def solution(mesh):
@@ -348,16 +373,17 @@
         in_vmem = pl.BlockSpec(memory_space=pltpu.VMEM)
         shard = jax.ShapeDtypeStruct((rows, width), F32)
         line = jax.ShapeDtypeStruct((1, rows), F32)
-        out = pl.pallas_call(
+        packed = pl.pallas_call(
             functools.partial(kernel, doms, chips, half),
-            out_shape=(shard, line, shard, line),
+            out_shape=jax.ShapeDtypeStruct((2 * rows + 8, wide), F32),
             in_specs=[in_vmem] * 4
             + [pl.BlockSpec(memory_space=pl.ANY), in_vmem, pl.BlockSpec(memory_space=pltpu.SMEM)]
             + [in_vmem] * 2,
-            out_specs=(in_vmem,) * 4,
+            out_specs=in_vmem,
             scratch_shapes=[
-                vm((nrel, width), F32),
-                vm((ep, wide), F32),
+                vm((width, nrel), F32),
+                vm((width, 128), F32),
+                vm((up(nrel, 128), wide), F32),
                 vm((2, ep, wide), F32),
                 vm((2, ep, ents), BF),
                 vm((2, ents, ep), BF),
@@ -385,12 +411,18 @@
             src_state.reshape(1, rows),
             dst_table,
             dst_state.reshape(1, rows),
-            relations,
+            relations.T,
             edge_src,
             edge_rel,
             edge_dst,
-            negatives.reshape(2, edges),
+            negatives,
         )
+        out = pl.pallas_call(
+            functools.partial(finish, half),
+            out_shape=(shard, line, shard, line),
+            in_specs=[in_vmem],
+            out_specs=(in_vmem,) * 4,
+        )(packed)
         return out[0], out[1].reshape(rows), out[2], out[3].reshape(rows)
 
     return jax.shard_map(

time: 74.3 us -> 60.7 us (0.82)
  local copies, waits for them, and re-layouts: 14.9 us -> 0 us
  Pallas kernels: 58.2 us -> 59.9 us
    unnamed x6 -> x0, local copies, waits for them, and re-layouts: 14.9 us -> none
    pallas_call x1 -> x2, Pallas kernels: 58.2 us -> 59.9 us  [the longest x1 58.3 us: on_device(): pl.pallas_call(functools.partial(kernel, doms, chips, half), out_shape=ja...]
where the time goes in v1:
time: 60.7 us; the launch traced here: 60.5 us
  Pallas kernels  59.9 us (99%)
  between operations  0.64 us (1%)
    pallas_call x1, Pallas kernels, on_device(): pl.pallas_call(functools.partial(kernel, doms, chips, half), out_shape=ja...  58.3 us
    pallas_call x1, Pallas kernels, on_device(): pl.pallas_call(functools.partial(finish, half), out_shape=(shard, line, s...  1.6 us

profile of v1, /device:TPU:1, one launch (start us, length us, event | category | flops | bytes accessed | tf_op | source)
XLA Modules:
  0.0 60.5 jit_solution(10380635688548551506)
XLA Ops:
  0.6 58.3 %shard_map.120.res_ref = f32[40,512]{1,0:T(8,128)} custom-call(f32[16,400]{1,0:T(8,128)} %src_ref.1, f32[1,16]{1,0:T(1,128)} %bitcast.6, f32[16,400]{1,0:T(8,128)} %dst_ref.1, f32[1,16]{1,0:T(1,128)} %bitcast.7, f32[400,4131]{1,0:T(8,128)} %bitcast.5, s32[2,500]{1,0:T(2,128)} %es_ref.1, s32[2,500]{1,0:T(2,128)} %er_ref.1, s32[2,500]{1,0:T(2,128)} %ed_ref.1, ...), custom_call_target="tpu_custom_call" | custom-call | tf_op jit(solution)/shard_map/pallas_call | solution.py:376
  58.9 1.6 %shard_map.121 = (f32[16,400]{1,0:T(8,128)}, f32[1,16]{1,0:T(1,128)}, f32[16,400]{1,0:T(8,128)}, f32[1,16]{1,0:T(1,128)}) custom-call(f32[40,512]{1,0:T(8,128)} %shard_map.120.res_ref), custom_call_target="tpu_custom_call" | custom-call | tf_op jit(solution)/shard_map/pallas_call | solution.py:420

commit v2 on v1

--- a/solution.py
+++ b/solution.py
@@ -10,6 +10,7 @@
 MESH = pl.DeviceIdType.MESH
 LEARN_RATE = 0.1
 EPSILON = 1e-06
+MSG = 50
 BF = jnp.bfloat16
 F32 = jnp.float32
 
@@ -31,22 +32,69 @@
     return lax.dot_general(a, b, (((1,), (1,)), ((), ())), preferred_element_type=F32)
 
 
+def lanes(n):
+    return lax.broadcasted_iota(jnp.int32, (n, 128), 1)
+
+
+def packed_rows(x):
+    a0, a1, b0, b1 = (x[:, n * 128:(n + 1) * 128] for n in range(4))
+    lane = lanes(x.shape[0])
+    both = jnp.where(lane < 64, a1, pltpu.roll(b1, 64, axis=1))
+    left = jnp.where(lane < 8, pltpu.roll(a1, 64, axis=1), jnp.where(lane < 16, pltpu.roll(b1, 72, axis=1), 0.0))
+    for n in (16, 32, 64):
+        left = left + pltpu.roll(left, n, axis=1)
+    line = lax.rem(lax.broadcasted_iota(jnp.int32, lane.shape, 0), 8)
+    left = jnp.where(lax.div(lane, 16) == 7 - line, left, 0.0)
+    tails = [jnp.sum(left[t:t + 8], axis=0, keepdims=True) for t in range(0, x.shape[0], 8)]
+    return a0, b0, both, tails
+
+
+def put_packed(ref, x):
+    a0, b0, both, tails = packed_rows(x)
+    n = x.shape[0]
+    ref[0:n] = a0
+    ref[n:2 * n] = b0
+    ref[2 * n:3 * n] = both
+    for t, row in enumerate(tails):
+        ref[3 * n + t:3 * n + t + 1] = row
+
+
+def unpacked(x, tails):
+    n = x.shape[0] // 3
+    lane = lanes(n)
+    a0, b0, both = x[0:n], x[n:2 * n], x[2 * n:3 * n]
+    re = []
+    for row in tails:
+        v = jnp.broadcast_to(pltpu.roll(row, 80, axis=1), (8, 128))
+        re.append(pltpu.roll(v, 0, axis=1, stride=16, stride_axis=0))
+    re = jnp.concatenate(re, axis=0)
+    im = pltpu.roll(re, 120, axis=1)
+    a1 = jnp.where(lane < 64, both, jnp.where(lane < 72, re, 0.0))
+    b1 = jnp.where(lane < 64, pltpu.roll(both, 64, axis=1), jnp.where(lane < 72, im, 0.0))
+    return jnp.concatenate([a0, a1, b0, b1], axis=1)
+
+
+def tail_rows(x_ref, n):
+    return [x_ref[3 * n + t:3 * n + t + 1] for t in range(n // 8)]
+
+
 def kernel(
     doms, chips, half,
-    src_ref, sst_ref, dst_ref, dstt_ref, rel_hbm, es_ref, er_ref, ed_ref, ng_ref,
+    src_hbm, sst_hbm, dst_hbm, dstt_hbm, rel_hbm, es_hbm, er_hbm, ed_hbm, ng_hbm,
     out_ref,
+    src_ref, sst_ref, dst_ref, dstt_ref, es_ref, er_ref, ed_ref, ng_ref,
     rel_t, rel_e, rel_v, rsp, hot, hot_t, wgt, pos, ids,
-    own_s, own_d, full_s, full_d, part_s, part_d, sib_s, sib_d, sum_s, sum_d, red_s, red_d,
+    tab_s, tab_d, own_s, own_d, full_s, full_d, part_s, part_d, sib_s, sib_d, sum_s, sum_d, red_s, red_d,
     qh, ql, dh, dl, th, tl, wth, wtl, wh, wl,
-    rel_sem, ags_send, ags_recv, agd_send, agd_recv, fws_send, fws_recv, fwd_send, fwd_recv,
+    in_sem, rel_sem, ags_send, ags_recv, agd_send, agd_recv, fws_send, fws_recv, fwd_send, fwd_recv,
     dd_send, dd_recv, rss_send, rss_recv, rsd_send, rsd_recv,
 ):
-    rows = src_ref.shape[0]
-    width = src_ref.shape[1]
+    rows, width = src_ref.shape
     hp = up(half, 128)
     wide = 2 * hp
-    ents = full_s.shape[1]
+    ents = th.shape[0]
     hent = ents // 2
+    shards = rows // 16
     edges = es_ref.shape[1]
     ep = rsp.shape[1]
     nrel = rel_hbm.shape[1]
@@ -57,13 +105,39 @@
     core = lax.rem(k, 2)
     chip = lax.div(k, 2)
     mate = chip * 2 + (1 - core)
+    nx = chips // 2
 
     def at_dom(step):
         return lax.rem(dom + step + doms, doms)
 
-    def peer(j):
-        return lax.rem(chip + j, chips)
-
+    def far(o):
+        return min(o[0], nx - o[0]) + 2 * o[1]
+
+    offsets = sorted(((dx, dy) for dx in range(nx) for dy in range(2)), key=lambda o: -far(o))
+    others = [o for o in offsets if o != (0, 0)]
+
+    def peer(o):
+        return lax.rem(lax.div(chip, 2) + o[0], nx) * 2 + lax.rem(lax.rem(chip, 2) + o[1], 2)
+
+    bar = pltpu.get_barrier_semaphore()
+    count = 1
+    for other in (at_dom(1), at_dom(-1)):
+        for o in offsets:
+            pl.semaphore_signal(bar, inc=1, device_id=(other, peer(o) * 2 + core), device_id_type=MESH)
+            count += 1
+    for o in others:
+        pl.semaphore_signal(bar, inc=1, device_id=(dom, peer(o) * 2 + core), device_id_type=MESH)
+        count += 1
+    pl.semaphore_signal(bar, inc=1, device_id=(dom, mate), device_id_type=MESH)
+
+    inputs = []
+    for n, (a, b) in enumerate((
+        (src_hbm, src_ref), (dst_hbm, dst_ref), (sst_hbm, sst_ref), (dstt_hbm, dstt_ref),
+        (es_hbm, es_ref), (er_hbm, er_ref), (ed_hbm, ed_ref), (ng_hbm, ng_ref),
+    )):
+        c = pltpu.make_async_copy(a, b, in_sem.at[n])
+        c.start()
+        inputs.append(c)
     piece = up(-(-width // rel_sem.shape[0]), 8)
     rel_copies = []
     for n in range(rel_sem.shape[0]):
@@ -75,28 +149,24 @@
             c.start()
             rel_copies.append(c)
 
-    bar = pltpu.get_barrier_semaphore()
-    count = 1
-    pl.semaphore_signal(bar, inc=1, device_id=(dom, mate), device_id_type=MESH)
-    for j in range(1, chips):
-        pl.semaphore_signal(bar, inc=1, device_id=(dom, peer(j) * 2 + core), device_id_type=MESH)
-        count += 1
-    for other in (at_dom(1), at_dom(-1)):
-        for j in range(chips):
-            pl.semaphore_signal(bar, inc=1, device_id=(other, peer(j) * 2 + core), device_id_type=MESH)
-            count += 1
-
     lane = lax.broadcasted_iota(jnp.int32, (rows, wide), 1)
 
-    def spread(x_ref, to):
-        to[0] = jnp.zeros((rows, wide), F32)
-        to[0, :, 0:width] = x_ref[...]
-        x = to[0]
+    def put_table(step, table, tab, own):
+        tab[step] = table
+        for n in range(shards):
+            put_packed(own.at[step, n], table[n * 16:n * 16 + 16])
+
+    def spread(x_ref, tab, own):
+        tab[0] = jnp.zeros((rows, wide), F32)
+        tab[0, :, 0:width] = x_ref[...]
+        x = tab[0]
         im = pltpu.roll(x, shift, axis=1)
-        to[0] = jnp.where(lane < half, x, jnp.where(lane >= hp, im, 0.0))
-
-    spread(src_ref, own_s)
-    spread(dst_ref, own_d)
+        put_table(0, jnp.where(lane < half, x, jnp.where(lane >= hp, im, 0.0)), tab, own)
+
+    for c in inputs:
+        c.wait()
+    spread(src_ref, tab_s, own_s)
+    spread(dst_ref, tab_d, own_d)
 
     eye = lax.broadcasted_iota(jnp.int32, (rows, rows), 0) == lax.broadcasted_iota(jnp.int32, (rows, rows), 1)
 
@@ -109,45 +179,39 @@
     src_state = column(sst_ref)
     dst_state = column(dstt_ref)
 
-    my_rows = pl.ds(pl.multiple_of(core * hent + chip * rows, rows), rows)
-
-    def block_of(c):
-        return pl.ds(pl.multiple_of(core * hent + c * rows, rows), rows)
-
-    def mate_block_of(c):
-        return pl.ds(pl.multiple_of((1 - core) * hent + c * rows, rows), rows)
+    mine = core * chips + chip
 
     def gather_src(step):
         out = []
-        for j in list(range(1, chips)):
+        for n, o in enumerate(others):
             c = pltpu.make_async_remote_copy(
-                own_s.at[step], full_s.at[step, my_rows], ags_send.at[step, j], ags_recv.at[step, chip],
-                device_id=(dom, peer(j) * 2 + core), device_id_type=MESH)
+                own_s.at[step], full_s.at[step, mine], ags_send.at[step, n], ags_recv.at[step, chip],
+                device_id=(dom, peer(o) * 2 + core), device_id_type=MESH)
             c.start()
             out.append(c)
         c = pltpu.make_async_remote_copy(
-            own_s.at[step], full_s.at[step, my_rows], fws_send.at[step, chip], fws_recv.at[step, chip],
+            own_s.at[step], full_s.at[step, mine], fws_send.at[step, chip], fws_recv.at[step, chip],
             device_id=(dom, mate), device_id_type=MESH)
         c.start()
         out.append(c)
-        full_s[step, my_rows] = own_s[step]
+        full_s[step, mine] = own_s[step]
         return out
 
     def gather_dst(step):
         out = []
-        for j in range(chips):
+        for n, o in enumerate(offsets):
             c = pltpu.make_async_remote_copy(
-                own_d.at[step], full_d.at[step, my_rows], agd_send.at[step, j], agd_recv.at[step, chip],
-                device_id=(at_dom(step + 1), peer(j) * 2 + core), device_id_type=MESH)
+                own_d.at[step], full_d.at[step, mine], agd_send.at[step, n], agd_recv.at[step, chip],
+                device_id=(at_dom(step + 1), peer(o) * 2 + core), device_id_type=MESH)
             c.start()
             out.append(c)
         return out
 
-    def forward(step, full, recv, fsend, frecv, first):
+    def forward(step, full, recv, fsend, frecv, which):
         out = []
-        for j in range(first, chips):
-            c = peer(j)
-            blk = full.at[step, block_of(c)]
+        for o in reversed(which):
+            c = peer(o)
+            blk = full.at[step, core * chips + c]
             pltpu.make_async_copy(blk, blk, recv.at[step, c]).wait()
             f = pltpu.make_async_remote_copy(
                 blk, blk, fsend.at[step, c], frecv.at[step, c], device_id=(dom, mate), device_id_type=MESH)
@@ -157,7 +221,7 @@
 
     def from_mate(step, full, frecv):
         for c in range(chips):
-            blk = full.at[step, mate_block_of(c)]
+            blk = full.at[step, (1 - core) * chips + c]
             pltpu.make_async_copy(blk, blk, frecv.at[step, c]).wait()
 
     def place(x):
@@ -201,8 +265,7 @@
             ids[slot] = jnp.full((1, ep), -1, jnp.int32)
             ids[slot, :, 0:edges] = ref[step] if len(ref.shape) == 3 else ref[step:step + 1, :]
             x = ids[slot]
-            x = jnp.where(x < 0, -1, place(jnp.maximum(x, 0)))
-            return x
+            return jnp.where(x < 0, -1, place(jnp.maximum(x, 0)))
 
         xs, xd, xn = hots(es_ref, 0), hots(ed_ref, 1), hots(ng_ref, 2)
         for m in range(0, ents, 128):
@@ -215,12 +278,17 @@
             pos[step, m:m + 128] = d
             wgt[step, m:m + 128] = d + c
 
-    def split_to(ref, step, a, b):
-        for m in range(0, ents, 128):
-            a[m:m + 128], b[m:m + 128] = halves(ref[step, m:m + 128])
+    lower = pl.ds(pl.multiple_of(core * hent, hent), hent)
+    upper = pl.ds(pl.multiple_of((1 - core) * hent, hent), hent)
+
+    def split_to(full, step, side, a, b):
+        for c in range(chips):
+            for n in range(shards):
+                blk = full.at[step, side * chips + c, n]
+                at = pl.ds(pl.multiple_of(side * hent + c * rows + n * 16, 16), 16)
+                a[at], b[at] = halves(unpacked(blk[0:48], tail_rows(blk, 16)))
 
     def rotated(step):
-        split_to(full_s, step, th, tl)
         for m in range(0, ep, 128):
             o = hot[step, m:m + 128]
             s = nn(o, th[...]) + nn(o, tl[...])
@@ -229,17 +297,14 @@
             qh[m:m + 128, :hp], ql[m:m + 128, :hp] = halves(sr * rr - si * ri)
             qh[m:m + 128, hp:], ql[m:m + 128, hp:] = halves(sr * ri + si * rr)
 
-    def weights(step):
-        split_to(full_d, step, dh, dl)
-        for m in range(0, ents, 128):
-            a, b = dh[m:m + 128], dl[m:m + 128]
+    def weights(step, side):
+        for m in range(0, hent, 128):
+            at = pl.ds(pl.multiple_of(side * hent + m, 128), 128)
+            a, b = dh[at], dl[at]
             s = nt(a, qh[...]) + (nt(a, ql[...]) + nt(b, qh[...]))
-            w = jax.nn.sigmoid(s) * wgt[step, m:m + 128] - pos[step, m:m + 128]
-            wth[m:m + 128], wtl[m:m + 128] = halves(w)
-            wh[:, m:m + 128], wl[:, m:m + 128] = halves(w.T)
-
-    lower = pl.ds(pl.multiple_of(core * hent, hent), hent)
-    upper = pl.ds(pl.multiple_of((1 - core) * hent, hent), hent)
+            w = jax.nn.sigmoid(s) * wgt[step, at] - pos[step, at]
+            wth[at], wtl[at] = halves(w)
+            wh[:, at], wl[:, at] = halves(w.T)
 
     def dst_part(which):
         a, b = wth[which], wtl[which]
@@ -265,30 +330,36 @@
         c.start()
         return c
 
-    def to_owners(step, t, copy, mine, sib, total, red, send, recv, target, first):
+    def to_owners(step, copy, part, sib, total, red, send, recv, target, which):
         copy.wait_recv()
-        total[step] = mine + sib[step]
+        for c in range(chips):
+            for n in range(shards):
+                at = slice(c * rows + n * 16, c * rows + n * 16 + 16)
+                put_packed(total.at[step, c, n], part[at] + sib[step, at])
         out = []
-        for j in range(first, chips):
-            c = peer(j)
+        for n, o in enumerate(which):
+            c = peer(o)
             r = pltpu.make_async_remote_copy(
-                total.at[step, pl.ds(pl.multiple_of(c * rows, rows), rows)], red.at[step, chip],
-                send.at[step, j], recv.at[step, chip],
+                total.at[step, c], red.at[step, chip], send.at[step, n], recv.at[step, chip],
                 device_id=(target, c * 2 + core), device_id_type=MESH)
             r.start()
             out.append(r)
-        if first == 1:
-            red[step, chip] = total[step, pl.ds(pl.multiple_of(chip * rows, rows), rows)]
+        if len(which) < chips:
+            red[step, chip] = total[step, chip]
         return out
 
-    def arrived(step, red, recv, first):
-        for j in range(first, chips):
-            blk = red.at[step, peer(j)]
-            pltpu.make_async_copy(blk, blk, recv.at[step, peer(j)]).wait()
-        g = red[step, 0]
-        for c in range(1, chips):
-            g = g + red[step, c]
-        return g
+    def arrived(step, red, recv, which):
+        for o in reversed(which):
+            blk = red.at[step, peer(o)]
+            pltpu.make_async_copy(blk, blk, recv.at[step, peer(o)]).wait()
+        out = []
+        for n in range(shards):
+            g, tails = red[step, 0, n, 0:48], tail_rows(red.at[step, 0, n], 16)
+            for c in range(1, chips):
+                g = g + red[step, c, n, 0:48]
+                tails = [t + u for t, u in zip(tails, tail_rows(red.at[step, c, n], 16))]
+            out.append(unpacked(g, tails))
+        return out[0] if shards == 1 else jnp.concatenate(out, axis=0)
 
     def adagrad(table, state, g):
         state = state + jnp.sum(g * g, axis=1, keepdims=True) / width
@@ -305,35 +376,44 @@
     prepare(0)
 
     for step in range(2):
-        sent += forward(step, full_s, ags_recv, fws_send, fws_recv, 1)
-        sent += forward(step, full_d, agd_recv, fwd_send, fwd_recv, 0)
+        if step == 0:
+            sent += forward(step, full_s, ags_recv, fws_send, fws_recv, others)
+            sent += forward(step, full_d, agd_recv, fwd_send, fwd_recv, offsets)
+        else:
+            sent += forward(step, full_d, agd_recv, fwd_send, fwd_recv, offsets)
+            sent += forward(step, full_s, ags_recv, fws_send, fws_recv, others)
+        split_to(full_s, step, core, th, tl)
         from_mate(step, full_s, fws_recv)
+        split_to(full_s, step, 1 - core, th, tl)
         rotated(step)
+        split_to(full_d, step, core, dh, dl)
+        weights(step, core)
         from_mate(step, full_d, fwd_recv)
-        weights(step)
+        split_to(full_d, step, 1 - core, dh, dl)
+        weights(step, 1 - core)
         part_d[step] = dst_part(upper)
         cd = to_mate(step, 0, part_d, sib_d)
         mine_d = dst_part(lower)
-        sent += to_owners(step, 0, cd, mine_d, sib_d, sum_d, red_d, rsd_send, rsd_recv, at_dom(-step - 1), 0)
+        sent += to_owners(step, cd, mine_d, sib_d, sum_d, red_d, rsd_send, rsd_recv, at_dom(-step - 1), offsets)
         edge_grads(step)
         part_s[step] = src_part(step, upper)
         cs = to_mate(step, 1, part_s, sib_s)
         mine_s = src_part(step, lower)
-        sent += to_owners(step, 1, cs, mine_s, sib_s, sum_s, red_s, rss_send, rss_recv, dom, 1)
+        sent += to_owners(step, cs, mine_s, sib_s, sum_s, red_s, rss_send, rss_recv, dom, others)
         if step == 0:
             prepare(1)
-        g = arrived(step, red_d, rsd_recv, 0)
-        table, dst_state = adagrad(own_d[step], dst_state, g)
+        g = arrived(step, red_d, rsd_recv, offsets)
+        table, dst_state = adagrad(tab_d[step], dst_state, g)
         if step == 0:
-            own_d[1] = table
+            put_table(1, table, tab_d, own_d)
             sent += gather_dst(1)
         else:
             out_ref[rows:2 * rows] = table
             out_ref[2 * rows + 1:2 * rows + 2, 0:rows] = as_row(dst_state)
-        g = arrived(step, red_s, rss_recv, 1)
-        table, src_state = adagrad(own_s[step], src_state, g)
+        g = arrived(step, red_s, rss_recv, others)
+        table, src_state = adagrad(tab_s[step], src_state, g)
         if step == 0:
-            own_s[1] = table
+            put_table(1, table, tab_s, own_s)
             sent += gather_src(1)
         else:
             out_ref[0:rows] = table
@@ -371,16 +451,25 @@
         nrel = relations.shape[0]
         vm, dma = pltpu.VMEM, pltpu.SemaphoreType.DMA
         in_vmem = pl.BlockSpec(memory_space=pltpu.VMEM)
+        in_hbm = pl.BlockSpec(memory_space=pltpu.HBM)
+        shards = rows // 16
+        block = (shards, MSG, 128)
         shard = jax.ShapeDtypeStruct((rows, width), F32)
         line = jax.ShapeDtypeStruct((1, rows), F32)
         packed = pl.pallas_call(
             functools.partial(kernel, doms, chips, half),
             out_shape=jax.ShapeDtypeStruct((2 * rows + 8, wide), F32),
-            in_specs=[in_vmem] * 4
-            + [pl.BlockSpec(memory_space=pl.ANY), in_vmem, pl.BlockSpec(memory_space=pltpu.SMEM)]
-            + [in_vmem] * 2,
+            in_specs=[in_hbm] * 9,
             out_specs=in_vmem,
             scratch_shapes=[
+                vm((rows, width), F32),
+                vm((1, rows), F32),
+                vm((rows, width), F32),
+                vm((1, rows), F32),
+                vm((2, edges), jnp.int32),
+                pltpu.SMEM((2, edges), jnp.int32),
+                vm((2, edges), jnp.int32),
+                vm(negatives.shape, jnp.int32),
                 vm((width, nrel), F32),
                 vm((width, 128), F32),
                 vm((up(nrel, 128), wide), F32),
@@ -392,19 +481,20 @@
                 vm((3, 1, ep), jnp.int32),
             ]
             + [vm((2, rows, wide), F32)] * 2
-            + [vm((2, ents, wide), F32)] * 2
-            + [vm((2, ents // 2, wide), F32)] * 6
-            + [vm((2, chips, rows, wide), F32)] * 2
+            + [vm((2,) + block, F32)] * 2
+            + [vm((2, edge_axis) + block, F32)] * 2
+            + [vm((2, ents // 2, wide), F32)] * 4
+            + [vm((2, chips) + block, F32)] * 4
             + [vm((ep, wide), BF)] * 2
             + [vm((ents, wide), BF)] * 4
             + [vm((ents, ep), BF)] * 2
             + [vm((ep, ents), BF)] * 2
-            + [dma((8,))]
+            + [dma((8,))] * 2
             + [dma((2, chips))] * 8
             + [dma((2, 2))] * 2
             + [dma((2, chips))] * 4,
             compiler_params=pltpu.CompilerParams(
-                collective_id=0, has_side_effects=True, vmem_limit_bytes=60 * 1024 * 1024
+                collective_id=0, has_side_effects=True, vmem_limit_bytes=58 * 1024 * 1024
             ),
         )(
             src_table,
@@ -422,6 +512,7 @@
             out_shape=(shard, line, shard, line),
             in_specs=[in_vmem],
             out_specs=(in_vmem,) * 4,
+            compiler_params=pltpu.CompilerParams(vmem_limit_bytes=1024 * 1024),
         )(packed)
         return out[0], out[1].reshape(rows), out[2], out[3].reshape(rows)
 

time: 60.7 us -> 57.1 us (0.941)
  Pallas kernels: 59.9 us -> 55.4 us
  local copies, waits for them, and re-layouts: 0 us -> 0.88 us
    pallas_call x1, Pallas kernels: 58.3 us -> 54.7 us  [on_device(): pl.pallas_call(functools.partial(kernel, doms, chips, half), out_shape=ja...]
    pallas_call x1, Pallas kernels: 1.6 us -> 0.71 us  [on_device(): pl.pallas_call(functools.partial(finish, half), out_shape=(shard, line, s...]
    unnamed x0 -> x2, local copies, waits for them, and re-layouts: none -> 0.88 us
where the time goes in v2:
time: 57.1 us; the launch traced here: 57 us
  Pallas kernels  55.4 us (97%)
  local copies, waits for them, and re-layouts  0.88 us (2%)
  between operations  0.65 us (1%)
    pallas_call x1, Pallas kernels, on_device(): pl.pallas_call(functools.partial(kernel, doms, chips, half), out_shape=ja...  54.7 us

profile of v2, /device:TPU:1, one launch (start us, length us, event | category | flops | bytes accessed | tf_op | source)
XLA Modules:
  0.0 57.0 jit_solution(10821245194535604937)
XLA Ops:
  0.6 54.7 %shard_map.120.res_ref = f32[40,512]{1,0:T(8,128)} custom-call(f32[16,400]{1,0:T(8,128)} %src_hbm.1, f32[1,16]{1,0:T(1,128)} %bitcast.6, f32[16,400]{1,0:T(8,128)} %dst_hbm.1, f32[1,16]{1,0:T(1,128)} %bitcast.7, f32[400,4131]{1,0:T(8,128)} %bitcast.5, s32[2,500]{1,0:T(2,128)} %es_hbm.1, s32[2,500]{1,0:T(2,128)} %er_hbm.1, s32[2,500]{1,0:T(2,128)} %ed_hbm.1, ...), custom_call_target="tpu_custom_call" | custom-call | tf_op jit(solution)/shard_map/pallas_call | solution.py:459
  55.4 0.0 copy-start
  55.4 0.9 %copy-done = f32[40,512]{1,0:T(8,128)S(1)} copy-done((f32[40,512]{1,0:T(8,128)S(1)}, f32[40,512]{1,0:T(8,128)}, u32[]{:S(2)}) %copy-start) | copy-done | bytes 81944
  56.3 0.7 %shard_map.121 = (f32[16,400]{1,0:T(8,128)}, f32[1,16]{1,0:T(1,128)}, f32[16,400]{1,0:T(8,128)}, f32[1,16]{1,0:T(1,128)}) custom-call(f32[40,512]{1,0:T(8,128)S(1)} %copy-done), custom_call_target="tpu_custom_call" | custom-call | tf_op jit(solution)/shard_map/pallas_call | solution.py:510
Async XLA Ops:
  55.4 0.9 %copy-start = (f32[40,512]{1,0:T(8,128)S(1)}, f32[40,512]{1,0:T(8,128)}, u32[]{:S(2)}) copy-start(f32[40,512]{1,0:T(8,128)} %shard_map.120.res_ref) | copy-start | bytes 245764

commit v3 on v2

--- a/solution.py
+++ b/solution.py
@@ -163,7 +163,7 @@
         im = pltpu.roll(x, shift, axis=1)
         put_table(0, jnp.where(lane < half, x, jnp.where(lane >= hp, im, 0.0)), tab, own)
 
-    for c in inputs:
+    for c in inputs[:2]:
         c.wait()
     spread(src_ref, tab_s, own_s)
     spread(dst_ref, tab_d, own_d)
@@ -175,9 +175,6 @@
 
     def as_row(x):
         return jnp.sum(jnp.where(eye, jnp.broadcast_to(x, (rows, rows)), 0.0), axis=0, keepdims=True)
-
-    src_state = column(sst_ref)
-    dst_state = column(dstt_ref)
 
     mine = core * chips + chip
 
@@ -304,13 +301,15 @@
             s = nt(a, qh[...]) + (nt(a, ql[...]) + nt(b, qh[...]))
             w = jax.nn.sigmoid(s) * wgt[step, at] - pos[step, at]
             wth[at], wtl[at] = halves(w)
-            wh[:, at], wl[:, at] = halves(w.T)
 
     def dst_part(which):
         a, b = wth[which], wtl[which]
         return nn(a, qh[...]) + (nn(a, ql[...]) + nn(b, qh[...]))
 
     def edge_grads(step):
+        for m in range(0, ents, 128):
+            wh[:, m:m + 128] = wth[m:m + 128].T
+            wl[:, m:m + 128] = wtl[m:m + 128].T
         for m in range(0, ep, 128):
             a, b = wh[m:m + 128], wl[m:m + 128]
             g = nn(a, dh[...]) + (nn(a, dl[...]) + nn(b, dh[...]))
@@ -370,8 +369,10 @@
     sent = []
     sent += gather_src(0)
     sent += gather_dst(0)
-    for c in rel_copies:
+    for c in inputs[2:] + rel_copies:
         c.wait()
+    src_state = column(sst_ref)
+    dst_state = column(dstt_ref)
     turn_relations()
     prepare(0)
 
@@ -379,17 +380,25 @@
         if step == 0:
             sent += forward(step, full_s, ags_recv, fws_send, fws_recv, others)
             sent += forward(step, full_d, agd_recv, fwd_send, fwd_recv, offsets)
+            split_to(full_s, step, core, th, tl)
+            from_mate(step, full_s, fws_recv)
+            split_to(full_s, step, 1 - core, th, tl)
+            rotated(step)
+            split_to(full_d, step, core, dh, dl)
+            weights(step, core)
+            from_mate(step, full_d, fwd_recv)
+            split_to(full_d, step, 1 - core, dh, dl)
         else:
             sent += forward(step, full_d, agd_recv, fwd_send, fwd_recv, offsets)
+            split_to(full_d, step, core, dh, dl)
+            from_mate(step, full_d, fwd_recv)
+            split_to(full_d, step, 1 - core, dh, dl)
             sent += forward(step, full_s, ags_recv, fws_send, fws_recv, others)
-        split_to(full_s, step, core, th, tl)
-        from_mate(step, full_s, fws_recv)
-        split_to(full_s, step, 1 - core, th, tl)
-        rotated(step)
-        split_to(full_d, step, core, dh, dl)
-        weights(step, core)
-        from_mate(step, full_d, fwd_recv)
-        split_to(full_d, step, 1 - core, dh, dl)
+            split_to(full_s, step, core, th, tl)
+            from_mate(step, full_s, fws_recv)
+            split_to(full_s, step, 1 - core, th, tl)
+            rotated(step)
+            weights(step, core)
         weights(step, 1 - core)
         part_d[step] = dst_part(upper)
         cd = to_mate(step, 0, part_d, sib_d)
@@ -494,9 +503,10 @@
             + [dma((2, 2))] * 2
             + [dma((2, chips))] * 4,
             compiler_params=pltpu.CompilerParams(
-                collective_id=0, has_side_effects=True, vmem_limit_bytes=58 * 1024 * 1024
+                collective_id=0, has_side_effects=True, vmem_limit_bytes=50 * 1024 * 1024
             ),
         )(
+            *(pltpu.with_memory_space_constraint(a, pltpu.HBM) for a in (
             src_table,
             src_state.reshape(1, rows),
             dst_table,
@@ -506,6 +516,7 @@
             edge_rel,
             edge_dst,
             negatives,
+            )),
         )
         out = pl.pallas_call(
             functools.partial(finish, half),

time: 57.1 us -> 55.7 us (0.975)
  local copies, waits for them, and re-layouts: 0.88 us -> 0 us
    unnamed x2 -> x0, local copies, waits for them, and re-layouts: 0.88 us -> none
where the time goes in v3:
time: 55.7 us; the launch traced here: 55.6 us
  Pallas kernels  54.9 us (99%)
  between operations  0.64 us (1%)
    pallas_call x1, Pallas kernels, on_device(): pl.pallas_call(functools.partial(kernel, doms, chips, half), out_shape=ja...  54.2 us

profile of v3, /device:TPU:1, one launch (start us, length us, event | category | flops | bytes accessed | tf_op | source)
XLA Modules:
  0.0 55.6 jit_solution(3946410021003486591)
XLA Ops:
  0.6 54.2 %shard_map.120.res_ref = f32[40,512]{1,0:T(8,128)S(1)} custom-call(f32[16,400]{1,0:T(8,128)} %src_hbm.1, f32[1,16]{1,0:T(1,128)} %bitcast.6, f32[16,400]{1,0:T(8,128)} %dst_hbm.1, f32[1,16]{1,0:T(1,128)} %bitcast.7, f32[400,4131]{1,0:T(8,128)} %bitcast.5, s32[2,500]{1,0:T(2,128)} %es_hbm.1, s32[2,500]{1,0:T(2,128)} %er_hbm.1, s32[2,500]{1,0:T(2,128)} %ed_hbm.1, ...), custom_call_target="tpu_custom_call" | custom-call | tf_op jit(solution)/shard_map/pallas_call | solution.py:468
  54.9 0.7 %shard_map.121 = (f32[16,400]{1,0:T(8,128)}, f32[1,16]{1,0:T(1,128)}, f32[16,400]{1,0:T(8,128)}, f32[1,16]{1,0:T(1,128)}) custom-call(f32[40,512]{1,0:T(8,128)S(1)} %shard_map.120.res_ref), custom_call_target="tpu_custom_call" | custom-call | tf_op jit(solution)/shard_map/pallas_call | solution.py:521

commit v4 on v3

--- a/solution.py
+++ b/solution.py
@@ -398,15 +398,16 @@
             from_mate(step, full_s, fws_recv)
             split_to(full_s, step, 1 - core, th, tl)
             rotated(step)
-            weights(step, core)
         weights(step, 1 - core)
         part_d[step] = dst_part(upper)
         cd = to_mate(step, 0, part_d, sib_d)
+        if step == 1:
+            weights(step, core)
         mine_d = dst_part(lower)
-        sent += to_owners(step, cd, mine_d, sib_d, sum_d, red_d, rsd_send, rsd_recv, at_dom(-step - 1), offsets)
         edge_grads(step)
         part_s[step] = src_part(step, upper)
         cs = to_mate(step, 1, part_s, sib_s)
+        sent += to_owners(step, cd, mine_d, sib_d, sum_d, red_d, rsd_send, rsd_recv, at_dom(-step - 1), offsets)
         mine_s = src_part(step, lower)
         sent += to_owners(step, cs, mine_s, sib_s, sum_s, red_s, rss_send, rss_recv, dom, others)
         if step == 0:

time: 55.7 us -> 54.7 us (0.982)
  Pallas kernels: 54.9 us -> 53.9 us
    pallas_call x1, Pallas kernels: 54.2 us -> 53.2 us  [on_device(): pl.pallas_call(functools.partial(kernel, doms, chips, half), out_shape=ja...]
where the time goes in v4:
time: 54.7 us; the launch traced here: 54.6 us
  Pallas kernels  53.9 us (99%)
  between operations  0.64 us (1%)
    pallas_call x1, Pallas kernels, on_device(): pl.pallas_call(functools.partial(kernel, doms, chips, half), out_shape=ja...  53.2 us

profile of v4, /device:TPU:1, one launch (start us, length us, event | category | flops | bytes accessed | tf_op | source)
XLA Modules:
  0.0 54.6 jit_solution(16598361217652165413)
XLA Ops:
  0.6 53.2 %shard_map.120.res_ref = f32[40,512]{1,0:T(8,128)S(1)} custom-call(f32[16,400]{1,0:T(8,128)} %src_hbm.1, f32[1,16]{1,0:T(1,128)} %bitcast.6, f32[16,400]{1,0:T(8,128)} %dst_hbm.1, f32[1,16]{1,0:T(1,128)} %bitcast.7, f32[400,4131]{1,0:T(8,128)} %bitcast.5, s32[2,500]{1,0:T(2,128)} %es_hbm.1, s32[2,500]{1,0:T(2,128)} %er_hbm.1, s32[2,500]{1,0:T(2,128)} %ed_hbm.1, ...), custom_call_target="tpu_custom_call" | custom-call | tf_op jit(solution)/shard_map/pallas_call | solution.py:469
  53.9 0.7 %shard_map.121 = (f32[16,400]{1,0:T(8,128)}, f32[1,16]{1,0:T(1,128)}, f32[16,400]{1,0:T(8,128)}, f32[1,16]{1,0:T(1,128)}) custom-call(f32[40,512]{1,0:T(8,128)S(1)} %shard_map.120.res_ref), custom_call_target="tpu_custom_call" | custom-call | tf_op jit(solution)/shard_map/pallas_call | solution.py:522

commit v5 on v4

--- a/solution.py
+++ b/solution.py
@@ -299,7 +299,7 @@
             at = pl.ds(pl.multiple_of(side * hent + m, 128), 128)
             a, b = dh[at], dl[at]
             s = nt(a, qh[...]) + (nt(a, ql[...]) + nt(b, qh[...]))
-            w = jax.nn.sigmoid(s) * wgt[step, at] - pos[step, at]
+            w = (0.5 * jnp.tanh(0.5 * s) + 0.5) * wgt[step, at] - pos[step, at]
             wth[at], wtl[at] = halves(w)
 
     def dst_part(which):
@@ -367,8 +367,8 @@
     pl.semaphore_wait(bar, count)
 
     sent = []
+    sent += gather_dst(0)
     sent += gather_src(0)
-    sent += gather_dst(0)
     for c in inputs[2:] + rel_copies:
         c.wait()
     src_state = column(sst_ref)
@@ -390,11 +390,11 @@
             split_to(full_d, step, 1 - core, dh, dl)
         else:
             sent += forward(step, full_d, agd_recv, fwd_send, fwd_recv, offsets)
+            sent += forward(step, full_s, ags_recv, fws_send, fws_recv, others)
+            split_to(full_s, step, core, th, tl)
             split_to(full_d, step, core, dh, dl)
             from_mate(step, full_d, fwd_recv)
             split_to(full_d, step, 1 - core, dh, dl)
-            sent += forward(step, full_s, ags_recv, fws_send, fws_recv, others)
-            split_to(full_s, step, core, th, tl)
             from_mate(step, full_s, fws_recv)
             split_to(full_s, step, 1 - core, th, tl)
             rotated(step)

time: 54.7 us -> 53.4 us (0.976); the launches traced: 54.6 us -> 52.6 us
  Pallas kernels: 53.9 us -> 52 us
    pallas_call x1, Pallas kernels: 53.2 us -> 51.3 us  [on_device(): pl.pallas_call(functools.partial(kernel, doms, chips, half), out_shape=ja...]
where the time goes in v5:
time: 53.4 us; the launch traced here: 52.6 us
  Pallas kernels  52 us (97%)
  between operations  0.64 us (1%)
    pallas_call x1, Pallas kernels, on_device(): pl.pallas_call(functools.partial(kernel, doms, chips, half), out_shape=ja...  51.3 us

profile of v5, /device:TPU:1, one launch (start us, length us, event | category | flops | bytes accessed | tf_op | source)
XLA Modules:
  0.0 52.6 jit_solution(2141963366095696145)
XLA Ops:
  0.6 51.3 %shard_map.120.res_ref = f32[40,512]{1,0:T(8,128)S(1)} custom-call(f32[16,400]{1,0:T(8,128)} %src_hbm.1, f32[1,16]{1,0:T(1,128)} %bitcast.6, f32[16,400]{1,0:T(8,128)} %dst_hbm.1, f32[1,16]{1,0:T(1,128)} %bitcast.7, f32[400,4131]{1,0:T(8,128)} %bitcast.5, s32[2,500]{1,0:T(2,128)} %es_hbm.1, s32[2,500]{1,0:T(2,128)} %er_hbm.1, s32[2,500]{1,0:T(2,128)} %ed_hbm.1, ...), custom_call_target="tpu_custom_call" | custom-call | tf_op jit(solution)/shard_map/pallas_call | solution.py:469
  51.9 0.7 %shard_map.121 = (f32[16,400]{1,0:T(8,128)}, f32[1,16]{1,0:T(1,128)}, f32[16,400]{1,0:T(8,128)}, f32[1,16]{1,0:T(1,128)}) custom-call(f32[40,512]{1,0:T(8,128)S(1)} %shard_map.120.res_ref), custom_call_target="tpu_custom_call" | custom-call | tf_op jit(solution)/shard_map/pallas_call | solution.py:522

commit v6 on v5

--- a/solution.py
+++ b/solution.py
@@ -381,10 +381,10 @@
             sent += forward(step, full_s, ags_recv, fws_send, fws_recv, others)
             sent += forward(step, full_d, agd_recv, fwd_send, fwd_recv, offsets)
             split_to(full_s, step, core, th, tl)
+            split_to(full_d, step, core, dh, dl)
             from_mate(step, full_s, fws_recv)
             split_to(full_s, step, 1 - core, th, tl)
             rotated(step)
-            split_to(full_d, step, core, dh, dl)
             weights(step, core)
             from_mate(step, full_d, fwd_recv)
             split_to(full_d, step, 1 - core, dh, dl)

time: 53.4 us -> 53.4 us (level)
  no operation moved by 1% of the time
where the time goes in v6:
time: 53.4 us; the launch traced here: 52.6 us
  Pallas kernels  52 us (97%)
  between operations  0.64 us (1%)
    pallas_call x1, Pallas kernels, on_device(): pl.pallas_call(functools.partial(kernel, doms, chips, half), out_shape=ja...  51.3 us

profile of v6, /device:TPU:1, one launch (start us, length us, event | category | flops | bytes accessed | tf_op | source)
XLA Modules:
  0.0 52.6 jit_solution(117503800934017014)
XLA Ops:
  0.6 51.3 %shard_map.120.res_ref = f32[40,512]{1,0:T(8,128)S(1)} custom-call(f32[16,400]{1,0:T(8,128)} %src_hbm.1, f32[1,16]{1,0:T(1,128)} %bitcast.6, f32[16,400]{1,0:T(8,128)} %dst_hbm.1, f32[1,16]{1,0:T(1,128)} %bitcast.7, f32[400,4131]{1,0:T(8,128)} %bitcast.5, s32[2,500]{1,0:T(2,128)} %es_hbm.1, s32[2,500]{1,0:T(2,128)} %er_hbm.1, s32[2,500]{1,0:T(2,128)} %ed_hbm.1, ...), custom_call_target="tpu_custom_call" | custom-call | tf_op jit(solution)/shard_map/pallas_call | solution.py:469
  51.9 0.7 %shard_map.121 = (f32[16,400]{1,0:T(8,128)}, f32[1,16]{1,0:T(1,128)}, f32[16,400]{1,0:T(8,128)}, f32[1,16]{1,0:T(1,128)}) custom-call(f32[40,512]{1,0:T(8,128)S(1)} %shard_map.120.res_ref), custom_call_target="tpu_custom_call" | custom-call | tf_op jit(solution)/shard_map/pallas_call | solution.py:522
